TPU v7x, 32 devices: a whole 2x2x4 slice. The times are simulated.
32 devices in a mesh: band: 16 (over z, y, core), ga: 2 (over x).
Axes of the slice: x: 2, y: 2, z: 4, core: 2. Of those that a mesh axis runs over, the one named last changes fastest.
Arguments:
- orbitals: bfloat16 [2, 16, 160, 128], P(None, 'band', 'ga'), may hold values from -8 to 8, as said below
- potential: float32 [480, 480], P('ga'), may hold values from -2 to 2
- slot_sticks: int32 [160], replicated, may hold values from -1 to 126, as said below
- stick_entries: int32 [160, 128], replicated, may hold values from -1 to 126, as said below
Outputs:
- applied_orbitals: bfloat16 [2, 16, 160, 128], P(None, 'band', 'ga')
- correlation: float32 [2, 16, 16], replicated
- reduced_hamiltonian: float32 [2, 16, 16], replicated
Inputs may be any that keep to these rules, and one draw needn't show every extreme that they name: `slot_sticks`: every gx with |gx| < 64 is held by exactly one slot; the other slots hold -1. Slots t with t // 80 = d are those of index d of ga; on some index of ga all 80 slots hold sticks. `stick_entries`: row t lists, in some order, gz + 63 for every gz with gx^2 + gz^2 < 64^2, gx being the stick of slot t, then -1 to the end of the row; rows of empty slots are all -1. `orbitals`: entries where stick_entries is -1 carry values that are not used.
All inputs are finite; a program needn't handle non-finite values.
Results may differ from a plain program's by a relative error of at most 0.001.
Values may be sent and summed in bfloat16 or wider, within the bound.
A program may use at most 64 MiB of HBM per device.

v0:
```python
import jax
import jax.numpy as jnp
from jax import lax
from jax.sharding import PartitionSpec as P

TWO_PI = 6.283185307179586
HIGHEST_PRECISION = lax.Precision.HIGHEST


def phases(frequency, position, points):
    winding = frequency[:, None] * position[None, :] % points
    angles = winding.astype(jnp.float32) * (TWO_PI / points)
    return (jnp.cos(angles), jnp.sin(angles))


def stick_phases(slot_sticks, radius, points):
    frequency = slot_sticks - radius + 1
    x_cos, x_sin = phases(frequency, jnp.arange(points, dtype=jnp.int32), points)
    filled = (slot_sticks >= 0).astype(jnp.float32)[:, None]
    return (x_cos * filled, x_sin * filled)


def selector_table(entry_lists):
    width = entry_lists.shape[1]
    return (entry_lists[:, :, None] == jnp.arange(width, dtype=jnp.int32)[None, None, :]).astype(
        jnp.bfloat16
    )


def spread_entries(coeffs, selector):
    return jnp.einsum("cbsk,skp->cbsp", coeffs, selector, preferred_element_type=jnp.float32)


def pick_entries(spectra, selector):
    return jnp.einsum(
        "cbsp,skp->cbsk", spectra, selector.astype(jnp.float32), precision=HIGHEST_PRECISION
    )


def z_forward(spread, z_cos, z_sin):
    real_part = jnp.einsum(
        "bsp,pz->bsz", spread[0], z_cos, precision=HIGHEST_PRECISION
    ) - jnp.einsum("bsp,pz->bsz", spread[1], z_sin, precision=HIGHEST_PRECISION)
    imag_part = jnp.einsum(
        "bsp,pz->bsz", spread[0], z_sin, precision=HIGHEST_PRECISION
    ) + jnp.einsum("bsp,pz->bsz", spread[1], z_cos, precision=HIGHEST_PRECISION)
    return jnp.stack([real_part, imag_part])


def plane_work(columns, x_cos, x_sin, potential):
    field_real = jnp.einsum(
        "bsz,sx->bzx", columns[0], x_cos, precision=HIGHEST_PRECISION
    ) - jnp.einsum("bsz,sx->bzx", columns[1], x_sin, precision=HIGHEST_PRECISION)
    field_imag = jnp.einsum(
        "bsz,sx->bzx", columns[0], x_sin, precision=HIGHEST_PRECISION
    ) + jnp.einsum("bsz,sx->bzx", columns[1], x_cos, precision=HIGHEST_PRECISION)
    prod_real = potential[None] * field_real
    prod_imag = potential[None] * field_imag
    back_real = jnp.einsum(
        "bzx,sx->bsz", prod_real, x_cos, precision=HIGHEST_PRECISION
    ) + jnp.einsum("bzx,sx->bsz", prod_imag, x_sin, precision=HIGHEST_PRECISION)
    back_imag = jnp.einsum(
        "bzx,sx->bsz", prod_imag, x_cos, precision=HIGHEST_PRECISION
    ) - jnp.einsum("bzx,sx->bsz", prod_real, x_sin, precision=HIGHEST_PRECISION)
    return jnp.stack([back_real, back_imag])


def z_backward(gathered, z_cos, z_sin, points):
    real_part = jnp.einsum(
        "bsz,pz->bsp", gathered[0], z_cos, precision=HIGHEST_PRECISION
    ) + jnp.einsum("bsz,pz->bsp", gathered[1], z_sin, precision=HIGHEST_PRECISION)
    imag_part = jnp.einsum(
        "bsz,pz->bsp", gathered[1], z_cos, precision=HIGHEST_PRECISION
    ) - jnp.einsum("bsz,pz->bsp", gathered[0], z_sin, precision=HIGHEST_PRECISION)
    return jnp.stack([real_part, imag_part]) / float(points * points)


def kinetic_factor(sticks, entry_lists, radius):
    gx_value = sticks - radius + 1
    gz_value = entry_lists - radius + 1
    return ((gx_value * gx_value)[:, None] + gz_value * gz_value).astype(jnp.float32) / float(
        radius * radius
    )


def cross_products(left, right, scale):
    dims = (((1,), (1,)), ((), ()))
    real_part = lax.dot_general(
        left[0], right[0], dims, preferred_element_type=jnp.float32
    ) + lax.dot_general(left[1], right[1], dims, preferred_element_type=jnp.float32)
    imag_part = lax.dot_general(
        left[0], right[1], dims, preferred_element_type=jnp.float32
    ) - lax.dot_general(left[1], right[0], dims, preferred_element_type=jnp.float32)
    return jnp.stack([real_part, imag_part]) * scale


def body(orbitals, potential, slot_sticks, stick_entries):
    points = potential.shape[1]
    width = stick_entries.shape[1]
    radius = width // 2
    band_count = orbitals.shape[1]
    slot_count = orbitals.shape[2]
    ga_index = lax.axis_index("ga")
    own_first = ga_index * slot_count
    own_lists = lax.dynamic_slice_in_dim(stick_entries, own_first, slot_count, 0)
    own_sticks = lax.dynamic_slice_in_dim(slot_sticks, own_first, slot_count, 0)
    present = own_lists >= 0
    own_selector = selector_table(own_lists)
    masked = jnp.where(present[None, None], orbitals, jnp.zeros_like(orbitals))
    frequency = jnp.arange(width, dtype=jnp.int32) - radius + 1
    whole_cos, whole_sin = phases(frequency, jnp.arange(points, dtype=jnp.int32), points)
    x_cos, x_sin = stick_phases(slot_sticks, radius, points)
    columns = z_forward(spread_entries(orbitals, own_selector), whole_cos, whole_sin)
    planes_columns = lax.all_to_all(columns, "ga", split_axis=3, concat_axis=2, tiled=True)
    gathered = plane_work(planes_columns, x_cos, x_sin, potential)
    returned = lax.all_to_all(gathered, "ga", split_axis=2, concat_axis=3, tiled=True)
    spectra = z_backward(returned, whole_cos, whole_sin, points)
    applied = pick_entries(spectra, own_selector)
    kinetic = kinetic_factor(own_sticks, own_lists, radius)
    applied_orbitals = jnp.where(
        present[None, None],
        kinetic[None, None] * orbitals.astype(jnp.float32) + applied,
        jnp.float32(0.0),
    ).astype(jnp.bfloat16)
    scale = 1.0 / (4.0 * radius * radius)
    flat_psi = masked.reshape(2, band_count, -1)
    flat_h = applied_orbitals.reshape(2, band_count, -1)
    portion = lax.all_gather(masked, "band", axis=1, tiled=True)
    remote_psi = portion.reshape(2, portion.shape[1], -1)
    block = jnp.stack(
        [cross_products(remote_psi, flat_psi, scale), cross_products(remote_psi, flat_h, scale)]
    )
    summed = lax.psum(block, "ga")
    matrices = lax.all_gather(summed, "band", axis=3, tiled=True)
    return (applied_orbitals, matrices[0], matrices[1])


def solution(mesh):
    return jax.shard_map(
        body,
        mesh=mesh,
        in_specs=(P(None, "band", "ga", None), P("ga", None), P(), P()),
        out_specs=(P(None, "band", "ga", None), P(), P()),
        check_vma=False,
    )
```

profile of v0, /device:TPU:0, one launch (start us, length us, event | category | flops | bytes accessed | tf_op | source)
XLA Modules:
  0.0 106.6 jit_solution(10663238395581667539)
XLA Ops:
  2.3 3.0 %fusion.10 = f32[2,1,80,128]{3,0,2,1:T(2,128)S(1)} fusion(s32[80,128]{1,0:T(8,128)S(1)} %get-tuple-element.16, bf16[2,80,128]{2,1,0:T(8,128)(2,1)} %bitcast.158), kind=kOutput, calls=%fused_computation.17 | convolution fusion | flops 6553600 | bytes 163840 | tf_op jit(solution)/shard_map/cbsk,skp->cbsp/dot_general | solution.py:31
  5.3 1.3 %fusion.53 = f32[80,480]{1,0:T(8,128)S(1)} fusion(f32[80,128]{1,0:T(8,128)S(1)} %bitcast.156, s32[128]{0:T(128)S(1)} %iota_add_fusion), kind=kOutput, calls=%fused_computation.76 | convolution fusion | flops 59535360 | bytes 195072 | tf_op jit(solution)/shard_map/bsp,pz->bsz/dot_general | solution.py:41
  6.7 1.4 %fusion.57 = f32[80,480]{1,0:T(8,128)S(1)} fusion(f32[80,128]{1,0:T(8,128)S(1)} %bitcast.157, s32[128]{0:T(128)S(1)} %iota_add_fusion), kind=kOutput, calls=%fused_computation.77 | convolution fusion | flops 59535360 | bytes 195072 | tf_op jit(solution)/shard_map/bsp,pz->bsz/dot_general | solution.py:44
  8.1 1.4 %fusion.9 = f32[1,1,80,480]{3,2,1,0:T(8,128)S(1)} fusion(f32[80,480]{1,0:T(8,128)S(1)} %fusion.53, f32[80,128]{1,0:T(8,128)S(1)} %bitcast.154, s32[128]{0:T(128)S(1)} %iota_add_fusion), kind=kOutput, calls=%fused_computation.16 | convolution fusion | flops 59573760 | bytes 348672 | tf_op jit(solution)/shard_map/bsp,pz->bsz/dot_general | solution.py:43
  9.5 1.4 %fusion.8 = f32[1,1,80,480]{3,2,1,0:T(8,128)S(1)} fusion(f32[80,480]{1,0:T(8,128)S(1)} %fusion.57, f32[80,128]{1,0:T(8,128)S(1)} %bitcast.155, s32[128]{0:T(128)S(1)} %iota_add_fusion), kind=kOutput, calls=%fused_computation.14 | convolution fusion | flops 59573760 | bytes 348672 | tf_op jit(solution)/shard_map/bsp,pz->bsz/dot_general | solution.py:46
  11.9 4.4 %all-to-all-start = ((f32[2,1,80,480]{2,1,0,3:T(1,128)}), f32[2,1,80,480]{2,1,0,3:T(1,128)S(1)}, u32[]{:S(2)}, u32[]{:S(2)}) async-start(f32[2,1,80,480]{2,1,0,3:T(1,128)} %copy.37), calls=%async_computation | async-start | bytes 983040 | tf_op jit(solution)/shard_map/all_to_all | solution.py:114
  16.4 24.4 %all_gather.6 = bf16[2,16,80,128]{3,2,0,1:T(8,128)(2,1)S(1)} all-gather(bf16[2,1,80,128]{3,2,0,1:T(8,128)(2,1)S(1)} %copy.45), channel_id=1, replica_groups=mesh['band'=16,'ga'=2] {'band'}, dimensions={1}, use_global_device_ids=true | all-gather | bytes 696320 | tf_op jit(solution)/shard_map/all_gather | solution.py:128
  42.3 1.9 %fusion.40 = f32[240,480]{1,0:T(8,128)S(1)} fusion(f32[160,240]{1,0:T(8,128)S(1)} %bitcast.152, f32[160]{0:T(256)S(1)} %compare_convert_fusion, s32[160]{0:T(256)S(1)} %broadcast_add_fusion), kind=kOutput, calls=%fused_computation.65 | convolution fusion | flops 221952000 | bytes 615680 | tf_op jit(solution)/shard_map/bsz,sx->bzx/dot_general | solution.py:51
  44.2 1.9 %fusion.41 = f32[240,480]{1,0:T(8,128)S(1)} fusion(f32[160,240]{1,0:T(8,128)S(1)} %bitcast.153, f32[160]{0:T(256)S(1)} %compare_convert_fusion, s32[160]{0:T(256)S(1)} %broadcast_add_fusion), kind=kOutput, calls=%fused_computation.66 | convolution fusion | flops 221952000 | bytes 615680 | tf_op jit(solution)/shard_map/bsz,sx->bzx/dot_general | solution.py:54
  46.1 1.9 %fusion.5 = f32[240,480]{1,0:T(8,128)S(1)} fusion(f32[240,480]{1,0:T(8,128)S(1)} %copy-done, f32[240,480]{1,0:T(8,128)S(1)} %fusion.40, f32[160,240]{1,0:T(8,128)S(1)} %bitcast.139, f32[160]{0:T(256)S(1)} %compare_convert_fusion, s32[160]{0:T(256)S(1)} %broadcast_add_fusion), kind=kOutput, calls=%fused_computation.8 | convolution fusion | flops 222182400 | bytes 1537280 | tf_op jit(solution)/shard_map/bsz,sx->bzx/dot_general | solution.py:53
  48.0 1.9 %fusion.39 = f32[160,240]{1,0:T(8,128)S(1)} fusion(f32[240,480]{1,0:T(8,128)S(1)} %fusion.5, f32[160]{0:T(256)S(1)} %compare_convert_fusion, s32[160]{0:T(256)S(1)} %broadcast_add_fusion), kind=kOutput, calls=%fused_computation.64 | convolution fusion | flops 221952000 | bytes 615680 | tf_op jit(solution)/shard_map/bzx,sx->bsz/dot_general | solution.py:59
  49.9 1.9 %fusion.4 = f32[240,480]{1,0:T(8,128)S(1)} fusion(f32[240,480]{1,0:T(8,128)S(1)} %copy-done, f32[240,480]{1,0:T(8,128)S(1)} %fusion.41, f32[160,240]{1,0:T(8,128)S(1)} %bitcast.140, f32[160]{0:T(256)S(1)} %compare_convert_fusion, s32[160]{0:T(256)S(1)} %broadcast_add_fusion), kind=kOutput, calls=%fused_computation.6 | convolution fusion | flops 222182400 | bytes 1537280 | tf_op jit(solution)/shard_map/bsz,sx->bzx/dot_general | solution.py:56
  51.8 1.9 %fusion.38 = f32[160,240]{1,0:T(8,128)S(1)} fusion(f32[240,480]{1,0:T(8,128)S(1)} %fusion.4, f32[160]{0:T(256)S(1)} %compare_convert_fusion, s32[160]{0:T(256)S(1)} %broadcast_add_fusion), kind=kOutput, calls=%fused_computation.63 | convolution fusion | flops 221952000 | bytes 615680 | tf_op jit(solution)/shard_map/bzx,sx->bsz/dot_general | solution.py:62
  53.7 2.1 %fusion.7 = f32[1,1,160,240]{3,2,1,0:T(8,128)S(1)} fusion(f32[160,240]{1,0:T(8,128)S(1)} %fusion.39, f32[240,480]{1,0:T(8,128)S(1)} %fusion.4, f32[160]{0:T(256)S(1)} %compare_convert_fusion, s32[160]{0:T(256)S(1)} %broadcast_add_fusion), kind=kOutput, calls=%fused_computation.12 | convolution fusion | flops 221990400 | bytes 769280 | tf_op jit(solution)/shard_map/bzx,sx->bsz/dot_general | solution.py:61
  55.9 1.9 %fusion.6 = f32[1,1,160,240]{3,2,1,0:T(8,128)S(1)} fusion(f32[160,240]{1,0:T(8,128)S(1)} %fusion.38, f32[240,480]{1,0:T(8,128)S(1)} %fusion.5, f32[160]{0:T(256)S(1)} %compare_convert_fusion, s32[160]{0:T(256)S(1)} %broadcast_add_fusion), kind=kOutput, calls=%fused_computation.10 | convolution fusion | flops 221990400 | bytes 769280 | tf_op jit(solution)/shard_map/bzx,sx->bsz/dot_general | solution.py:64
  58.9 3.5 %all-to-all-start.1 = ((f32[2,1,160,240]{3,1,0,2:T(1,128)}), f32[2,1,160,240]{3,1,0,2:T(1,128)S(1)}, u32[]{:S(2)}, u32[]{:S(2)}) async-start(f32[2,1,160,240]{3,1,0,2:T(1,128)} %copy.41), calls=%async_computation.1 | async-start | bytes 655360 | tf_op jit(solution)/shard_map/all_to_all | solution.py:116
  62.8 6.5 %all-to-all-done.1 = f32[2,1,160,240]{3,1,0,2:T(1,128)S(1)} async-done(((f32[2,1,160,240]{3,1,0,2:T(1,128)}), f32[2,1,160,240]{3,1,0,2:T(1,128)S(1)}, u32[]{:S(2)}, u32[]{:S(2)}) %all-to-all-start.1) | async-done | bytes 307232 | tf_op jit(solution)/shard_map/all_to_all | solution.py:116
  70.0 1.4 %fusion.50 = f32[80,128]{1,0:T(8,128)S(1)} fusion(f32[80,480]{1,0:T(8,128)S(1)} %reshape.267, s32[128]{0:T(128)S(1)} %iota_add_fusion), kind=kOutput, calls=%fused_computation.75 | convolution fusion | flops 59535360 | bytes 195072 | tf_op jit(solution)/shard_map/bsz,pz->bsp/dot_general | solution.py:69
  71.6 1.4 %fusion.48 = f32[80,128]{1,0:T(8,128)S(1)} fusion(f32[80,480]{1,0:T(8,128)S(1)} %reshape.268, s32[128]{0:T(128)S(1)} %iota_add_fusion), kind=kOutput, calls=%fused_computation.74 | convolution fusion | flops 59535360 | bytes 195072 | tf_op jit(solution)/shard_map/bsz,pz->bsp/dot_general | solution.py:72
  73.0 1.4 %fusion.16 = f32[1,80,128]{2,1,0:T(8,128)S(1)} fusion(f32[80,128]{1,0:T(8,128)S(1)} %fusion.50, f32[80,480]{1,0:T(8,128)S(1)} %reshape.268, s32[128]{0:T(128)S(1)} %iota_add_fusion), kind=kOutput, calls=%fused_computation.25 | convolution fusion | flops 59545600 | bytes 236032 | tf_op jit(solution)/shard_map/bsz,pz->bsp/dot_general | solution.py:71
  74.5 1.5 %fusion.15 = f32[1,80,128]{2,1,0:T(8,128)S(1)} fusion(f32[80,128]{1,0:T(8,128)S(1)} %fusion.48, f32[80,480]{1,0:T(8,128)S(1)} %reshape.267, s32[128]{0:T(128)S(1)} %iota_add_fusion), kind=kOutput, calls=%fused_computation.23 | convolution fusion | flops 59545600 | bytes 236032 | tf_op jit(solution)/shard_map/bsz,pz->bsp/dot_general | solution.py:74
  76.0 5.6 %fusion.14 = bf16[2,1,80,128]{3,0,2,1:T(2,128)(2,1)S(1)} fusion(s32[80,128]{1,0:T(8,128)S(1)} %get-tuple-element.16, f32[2,80,128]{2,1,0:T(8,128)S(1)} %maximum_multiply_fusion, pred[80,128]{1,0:T(8,128)(4,1)S(1)} %broadcast_compare_fusion, f32[80,128]{1,0:T(8,128)S(1)} %get-tuple-element.15, bf16[2,1,80,128]{3,2,1,0:T(8,128)(2,1)S(1)} %copy-done.1), kind=kOutput, calls=%fused_computation.21 | convolution fusion | flops 32870400 | bytes 256000 | tf_op jit(solution)/shard_map/cbsp,skp->cbsk/dot_general | solution.py:35
  83.1 4.9 %psum.7 = f32[2,2,16,1]{2,3,1,0:T(1,128)S(1)} all-reduce(f32[2,2,16,1]{2,3,1,0:T(1,128)S(1)} %pad_maximum_fusion.2), channel_id=1, replica_groups=mesh['band'=16,'ga'=2] {'ga'}, use_global_device_ids=true, to_apply=%region_0.1 | all-reduce | flops 64 | bytes 512 | tf_op jit(solution)/shard_map/psum | solution.py:133
  88.1 17.2 %all_gather.7 = f32[2,2,16,16]{2,1,0,3:T(2,128)S(1)} all-gather(f32[2,2,16,1]{2,1,0,3:T(2,128)S(1)} %bitcast.159), channel_id=1, replica_groups=mesh['band'=16,'ga'=2] {'band'}, dimensions={3}, use_global_device_ids=true | all-gather | bytes 4352 | tf_op jit(solution)/shard_map/all_gather | solution.py:134
  (45 shorter events, 9.7 us)
Async XLA Ops:
  11.9 4.4 %copy-start.2 = (s32[160]{0:T(256)S(1)}, s32[160]{0:T(256)}, u32[]{:S(2)}) copy-start(s32[160]{0:T(256)} %param.6) | copy-start | bytes 1924
  11.9 4.4 %copy-start.1 = (bf16[2,1,80,128]{3,2,1,0:T(8,128)(2,1)S(1)}, bf16[2,1,80,128]{3,2,1,0:T(8,128)(2,1)}, u32[]{:S(2)}) copy-start(bf16[2,1,80,128]{3,2,1,0:T(8,128)(2,1)} %param.4) | copy-start | bytes 122884
  11.9 29.4 %all-to-all-start = ((f32[2,1,80,480]{2,1,0,3:T(1,128)}), f32[2,1,80,480]{2,1,0,3:T(1,128)S(1)}, u32[]{:S(2)}, u32[]{:S(2)}) async-start(f32[2,1,80,480]{2,1,0,3:T(1,128)} %copy.37), calls=%async_computation | async-start | bytes 983040 | tf_op jit(solution)/shard_map/all_to_all | solution.py:114
  44.2 1.9 %copy-start = (f32[240,480]{1,0:T(8,128)S(1)}, f32[240,480]{1,0:T(8,128)}, u32[]{:S(2)}) copy-start(f32[240,480]{1,0:T(8,128)} %param.5) | copy-start | bytes 1382404
  58.9 10.4 %all-to-all-start.1 = ((f32[2,1,160,240]{3,1,0,2:T(1,128)}), f32[2,1,160,240]{3,1,0,2:T(1,128)S(1)}, u32[]{:S(2)}, u32[]{:S(2)}) async-start(f32[2,1,160,240]{3,1,0,2:T(1,128)} %copy.41), calls=%async_computation.1 | async-start | bytes 655360 | tf_op jit(solution)/shard_map/all_to_all | solution.py:116
where the time goes:
time: 107 us
  blocking collectives  46.5 us (43%)
  matrix products  37 us (35%)
  starting transfers between devices  7.82 us (7%)
  waiting for transfers between devices  6.46 us (6%)
  local copies, waits for them, and re-layouts  6.1 us (6%)
  other arithmetic  1.8 us (2%)
    all_gather x1, blocking collectives, body(): portion = lax.all_gather(masked, 'band', axis=1, tiled=True)  24.4 us
    all_gather x1, blocking collectives, body(): matrices = lax.all_gather(summed, 'band', axis=3, tiled=True)  17.2 us
    all_to_all x1, waiting for transfers between devices, body(): lax.all_to_all(gathered, 'ga', split_axis=2, concat_axis=3, tiled=True)  6.46 us
    dot_general x1, matrix products, pick_entries(): jnp.einsum('cbsp,skp->cbsk', spectra, selector.astype(jnp.float32), preci...  5.62 us
    psum x1, blocking collectives, body(): summed = lax.psum(block, 'ga')  4.93 us
    all_to_all x1, starting transfers between devices, body(): lax.all_to_all(columns, 'ga', split_axis=3, concat_axis=2, tiled=True)  4.36 us
    all_to_all x1, starting transfers between devices, body(): lax.all_to_all(gathered, 'ga', split_axis=2, concat_axis=3, tiled=True)  3.45 us
    dot_general x1, matrix products, spread_entries(): jnp.einsum('cbsk,skp->cbsp', coeffs, selector, preferred_element_type=jnp...  3.01 us
  transfers between devices with their start and end apart: 2, of which 1 were waited for; matrix products, arithmetic and copies ran while one was open for 1% of the time, Pallas kernels for 0%

commit v1 on v0

--- a/solution.py
+++ b/solution.py
@@ -125,7 +125,7 @@
     scale = 1.0 / (4.0 * radius * radius)
     flat_psi = masked.reshape(2, band_count, -1)
     flat_h = applied_orbitals.reshape(2, band_count, -1)
-    portion = lax.all_gather(masked, "band", axis=1, tiled=True)
+    portion = jnp.concatenate(lax.all_gather(masked, "band"), axis=1)
     remote_psi = portion.reshape(2, portion.shape[1], -1)
     block = jnp.stack(
         [cross_products(remote_psi, flat_psi, scale), cross_products(remote_psi, flat_h, scale)]

time: 107 us -> 107 us (level)
  no operation moved by 1% of the time
where the time goes in v1:
time: 107 us
  blocking collectives  46.5 us (43%)
  matrix products  37 us (35%)
  starting transfers between devices  7.82 us (7%)
  waiting for transfers between devices  6.46 us (6%)
  local copies, waits for them, and re-layouts  6.1 us (6%)
  other arithmetic  1.8 us (2%)
    all_gather x1, blocking collectives, body(): portion = jnp.concatenate(lax.all_gather(masked, 'band'), axis=1)  24.4 us
    all_gather x1, blocking collectives, body(): matrices = lax.all_gather(summed, 'band', axis=3, tiled=True)  17.2 us
    all_to_all x1, waiting for transfers between devices, body(): lax.all_to_all(gathered, 'ga', split_axis=2, concat_axis=3, tiled=True)  6.46 us
    dot_general x1, matrix products, pick_entries(): jnp.einsum('cbsp,skp->cbsk', spectra, selector.astype(jnp.float32), preci...  5.62 us
    psum x1, blocking collectives, body(): summed = lax.psum(block, 'ga')  4.93 us
    all_to_all x1, starting transfers between devices, body(): lax.all_to_all(columns, 'ga', split_axis=3, concat_axis=2, tiled=True)  4.36 us
    all_to_all x1, starting transfers between devices, body(): lax.all_to_all(gathered, 'ga', split_axis=2, concat_axis=3, tiled=True)  3.45 us
    dot_general x1, matrix products, spread_entries(): jnp.einsum('cbsk,skp->cbsp', coeffs, selector, preferred_element_type=jnp...  3.01 us
  transfers between devices with their start and end apart: 2, of which 1 were waited for; matrix products, arithmetic and copies ran while one was open for 1% of the time, Pallas kernels for 0%

profile of v1, /device:TPU:0, one launch (start us, length us, event | category | flops | bytes accessed | tf_op | source)
XLA Modules:
  0.0 106.6 jit_solution(6374747203646818595)
XLA Ops:
  2.3 3.0 %fusion.10 = f32[2,1,80,128]{3,0,2,1:T(2,128)S(1)} fusion(s32[80,128]{1,0:T(8,128)S(1)} %get-tuple-element.16, bf16[2,80,128]{2,1,0:T(8,128)(2,1)} %bitcast.134), kind=kOutput, calls=%fused_computation.17 | convolution fusion | flops 6553600 | bytes 163840 | tf_op jit(solution)/shard_map/cbsk,skp->cbsp/dot_general | solution.py:31
  5.3 1.3 %fusion.45 = f32[80,480]{1,0:T(8,128)S(1)} fusion(f32[80,128]{1,0:T(8,128)S(1)} %bitcast.132, s32[128]{0:T(128)S(1)} %iota_add_fusion), kind=kOutput, calls=%fused_computation.70 | convolution fusion | flops 59535360 | bytes 195072 | tf_op jit(solution)/shard_map/bsp,pz->bsz/dot_general | solution.py:41
  6.7 1.4 %fusion.49 = f32[80,480]{1,0:T(8,128)S(1)} fusion(f32[80,128]{1,0:T(8,128)S(1)} %bitcast.133, s32[128]{0:T(128)S(1)} %iota_add_fusion), kind=kOutput, calls=%fused_computation.71 | convolution fusion | flops 59535360 | bytes 195072 | tf_op jit(solution)/shard_map/bsp,pz->bsz/dot_general | solution.py:44
  8.1 1.4 %fusion.9 = f32[1,1,80,480]{3,2,1,0:T(8,128)S(1)} fusion(f32[80,480]{1,0:T(8,128)S(1)} %fusion.45, f32[80,128]{1,0:T(8,128)S(1)} %bitcast.130, s32[128]{0:T(128)S(1)} %iota_add_fusion), kind=kOutput, calls=%fused_computation.16 | convolution fusion | flops 59573760 | bytes 348672 | tf_op jit(solution)/shard_map/bsp,pz->bsz/dot_general | solution.py:43
  9.5 1.4 %fusion.8 = f32[1,1,80,480]{3,2,1,0:T(8,128)S(1)} fusion(f32[80,480]{1,0:T(8,128)S(1)} %fusion.49, f32[80,128]{1,0:T(8,128)S(1)} %bitcast.131, s32[128]{0:T(128)S(1)} %iota_add_fusion), kind=kOutput, calls=%fused_computation.14 | convolution fusion | flops 59573760 | bytes 348672 | tf_op jit(solution)/shard_map/bsp,pz->bsz/dot_general | solution.py:46
  11.9 4.4 %all-to-all-start = ((f32[2,1,80,480]{2,1,0,3:T(1,128)}), f32[2,1,80,480]{2,1,0,3:T(1,128)S(1)}, u32[]{:S(2)}, u32[]{:S(2)}) async-start(f32[2,1,80,480]{2,1,0,3:T(1,128)} %copy.38), calls=%async_computation | async-start | bytes 983040 | tf_op jit(solution)/shard_map/all_to_all | solution.py:114
  16.4 24.4 %all-gather = bf16[32,1,80,128]{3,2,1,0:T(8,128)(2,1)S(1)} all-gather(bf16[2,1,80,128]{3,2,1,0:T(8,128)(2,1)S(1)} %copy.46), channel_id=2, replica_groups=mesh['band'=16,'ga'=2] {'band'}, dimensions={0}, use_global_device_ids=true | all-gather | bytes 696320 | tf_op jit(solution)/shard_map/all_gather | solution.py:128
  42.3 1.9 %fusion.32 = f32[240,480]{1,0:T(8,128)S(1)} fusion(f32[160,240]{1,0:T(8,128)S(1)} %bitcast.128, f32[160]{0:T(256)S(1)} %compare_convert_fusion, s32[160]{0:T(256)S(1)} %broadcast_add_fusion), kind=kOutput, calls=%fused_computation.59 | convolution fusion | flops 221952000 | bytes 615680 | tf_op jit(solution)/shard_map/bsz,sx->bzx/dot_general | solution.py:51
  44.2 1.9 %fusion.33 = f32[240,480]{1,0:T(8,128)S(1)} fusion(f32[160,240]{1,0:T(8,128)S(1)} %bitcast.129, f32[160]{0:T(256)S(1)} %compare_convert_fusion, s32[160]{0:T(256)S(1)} %broadcast_add_fusion), kind=kOutput, calls=%fused_computation.60 | convolution fusion | flops 221952000 | bytes 615680 | tf_op jit(solution)/shard_map/bsz,sx->bzx/dot_general | solution.py:54
  46.1 1.9 %fusion.5 = f32[240,480]{1,0:T(8,128)S(1)} fusion(f32[240,480]{1,0:T(8,128)S(1)} %copy-done, f32[240,480]{1,0:T(8,128)S(1)} %fusion.32, f32[160,240]{1,0:T(8,128)S(1)} %bitcast.123, f32[160]{0:T(256)S(1)} %compare_convert_fusion, s32[160]{0:T(256)S(1)} %broadcast_add_fusion), kind=kOutput, calls=%fused_computation.8 | convolution fusion | flops 222182400 | bytes 1537280 | tf_op jit(solution)/shard_map/bsz,sx->bzx/dot_general | solution.py:53
  48.0 1.9 %fusion.31 = f32[160,240]{1,0:T(8,128)S(1)} fusion(f32[240,480]{1,0:T(8,128)S(1)} %fusion.5, f32[160]{0:T(256)S(1)} %compare_convert_fusion, s32[160]{0:T(256)S(1)} %broadcast_add_fusion), kind=kOutput, calls=%fused_computation.58 | convolution fusion | flops 221952000 | bytes 615680 | tf_op jit(solution)/shard_map/bzx,sx->bsz/dot_general | solution.py:59
  49.9 1.9 %fusion.4 = f32[240,480]{1,0:T(8,128)S(1)} fusion(f32[240,480]{1,0:T(8,128)S(1)} %copy-done, f32[240,480]{1,0:T(8,128)S(1)} %fusion.33, f32[160,240]{1,0:T(8,128)S(1)} %bitcast.124, f32[160]{0:T(256)S(1)} %compare_convert_fusion, s32[160]{0:T(256)S(1)} %broadcast_add_fusion), kind=kOutput, calls=%fused_computation.6 | convolution fusion | flops 222182400 | bytes 1537280 | tf_op jit(solution)/shard_map/bsz,sx->bzx/dot_general | solution.py:56
  51.8 1.9 %fusion.30 = f32[160,240]{1,0:T(8,128)S(1)} fusion(f32[240,480]{1,0:T(8,128)S(1)} %fusion.4, f32[160]{0:T(256)S(1)} %compare_convert_fusion, s32[160]{0:T(256)S(1)} %broadcast_add_fusion), kind=kOutput, calls=%fused_computation.57 | convolution fusion | flops 221952000 | bytes 615680 | tf_op jit(solution)/shard_map/bzx,sx->bsz/dot_general | solution.py:62
  53.7 2.1 %fusion.7 = f32[1,1,160,240]{3,2,1,0:T(8,128)S(1)} fusion(f32[160,240]{1,0:T(8,128)S(1)} %fusion.31, f32[240,480]{1,0:T(8,128)S(1)} %fusion.4, f32[160]{0:T(256)S(1)} %compare_convert_fusion, s32[160]{0:T(256)S(1)} %broadcast_add_fusion), kind=kOutput, calls=%fused_computation.12 | convolution fusion | flops 221990400 | bytes 769280 | tf_op jit(solution)/shard_map/bzx,sx->bsz/dot_general | solution.py:61
  55.9 1.9 %fusion.6 = f32[1,1,160,240]{3,2,1,0:T(8,128)S(1)} fusion(f32[160,240]{1,0:T(8,128)S(1)} %fusion.30, f32[240,480]{1,0:T(8,128)S(1)} %fusion.5, f32[160]{0:T(256)S(1)} %compare_convert_fusion, s32[160]{0:T(256)S(1)} %broadcast_add_fusion), kind=kOutput, calls=%fused_computation.10 | convolution fusion | flops 221990400 | bytes 769280 | tf_op jit(solution)/shard_map/bzx,sx->bsz/dot_general | solution.py:64
  58.9 3.5 %all-to-all-start.1 = ((f32[2,1,160,240]{3,1,0,2:T(1,128)}), f32[2,1,160,240]{3,1,0,2:T(1,128)S(1)}, u32[]{:S(2)}, u32[]{:S(2)}) async-start(f32[2,1,160,240]{3,1,0,2:T(1,128)} %copy.42), calls=%async_computation.1 | async-start | bytes 655360 | tf_op jit(solution)/shard_map/all_to_all | solution.py:116
  62.8 6.5 %all-to-all-done.1 = f32[2,1,160,240]{3,1,0,2:T(1,128)S(1)} async-done(((f32[2,1,160,240]{3,1,0,2:T(1,128)}), f32[2,1,160,240]{3,1,0,2:T(1,128)S(1)}, u32[]{:S(2)}, u32[]{:S(2)}) %all-to-all-start.1) | async-done | bytes 307232 | tf_op jit(solution)/shard_map/all_to_all | solution.py:116
  70.0 1.4 %fusion.42 = f32[80,128]{1,0:T(8,128)S(1)} fusion(f32[80,480]{1,0:T(8,128)S(1)} %reshape.289, s32[128]{0:T(128)S(1)} %iota_add_fusion), kind=kOutput, calls=%fused_computation.69 | convolution fusion | flops 59535360 | bytes 195072 | tf_op jit(solution)/shard_map/bsz,pz->bsp/dot_general | solution.py:69
  71.6 1.4 %fusion.40 = f32[80,128]{1,0:T(8,128)S(1)} fusion(f32[80,480]{1,0:T(8,128)S(1)} %reshape.290, s32[128]{0:T(128)S(1)} %iota_add_fusion), kind=kOutput, calls=%fused_computation.68 | convolution fusion | flops 59535360 | bytes 195072 | tf_op jit(solution)/shard_map/bsz,pz->bsp/dot_general | solution.py:72
  73.0 1.4 %fusion.16 = f32[1,80,128]{2,1,0:T(8,128)S(1)} fusion(f32[80,128]{1,0:T(8,128)S(1)} %fusion.42, f32[80,480]{1,0:T(8,128)S(1)} %reshape.290, s32[128]{0:T(128)S(1)} %iota_add_fusion), kind=kOutput, calls=%fused_computation.25 | convolution fusion | flops 59545600 | bytes 236032 | tf_op jit(solution)/shard_map/bsz,pz->bsp/dot_general | solution.py:71
  74.5 1.5 %fusion.15 = f32[1,80,128]{2,1,0:T(8,128)S(1)} fusion(f32[80,128]{1,0:T(8,128)S(1)} %fusion.40, f32[80,480]{1,0:T(8,128)S(1)} %reshape.289, s32[128]{0:T(128)S(1)} %iota_add_fusion), kind=kOutput, calls=%fused_computation.23 | convolution fusion | flops 59545600 | bytes 236032 | tf_op jit(solution)/shard_map/bsz,pz->bsp/dot_general | solution.py:74
  76.0 5.6 %fusion.14 = bf16[2,1,80,128]{3,0,2,1:T(2,128)(2,1)S(1)} fusion(s32[80,128]{1,0:T(8,128)S(1)} %get-tuple-element.16, f32[2,80,128]{2,1,0:T(8,128)S(1)} %maximum_multiply_fusion, pred[80,128]{1,0:T(8,128)(4,1)S(1)} %broadcast_compare_fusion, f32[80,128]{1,0:T(8,128)S(1)} %get-tuple-element.15, bf16[2,1,80,128]{3,2,1,0:T(8,128)(2,1)S(1)} %copy-done.1), kind=kOutput, calls=%fused_computation.21 | convolution fusion | flops 32870400 | bytes 256000 | tf_op jit(solution)/shard_map/cbsp,skp->cbsk/dot_general | solution.py:35
  83.1 4.9 %psum.7 = f32[2,2,16,1]{2,3,1,0:T(1,128)S(1)} all-reduce(f32[2,2,16,1]{2,3,1,0:T(1,128)S(1)} %pad_maximum_fusion.2), channel_id=1, replica_groups=mesh['band'=16,'ga'=2] {'ga'}, use_global_device_ids=true, to_apply=%region_0.1 | all-reduce | flops 64 | bytes 512 | tf_op jit(solution)/shard_map/psum | solution.py:133
  88.1 17.2 %all_gather.11 = f32[2,2,16,16]{2,1,0,3:T(2,128)S(1)} all-gather(f32[2,2,16,1]{2,1,0,3:T(2,128)S(1)} %bitcast.135), channel_id=1, replica_groups=mesh['band'=16,'ga'=2] {'band'}, dimensions={3}, use_global_device_ids=true | all-gather | bytes 4352 | tf_op jit(solution)/shard_map/all_gather | solution.py:134
  (45 shorter events, 9.7 us)
Async XLA Ops:
  11.9 4.4 %copy-start.2 = (s32[160]{0:T(256)S(1)}, s32[160]{0:T(256)}, u32[]{:S(2)}) copy-start(s32[160]{0:T(256)} %param.6) | copy-start | bytes 1924
  11.9 4.4 %copy-start.1 = (bf16[2,1,80,128]{3,2,1,0:T(8,128)(2,1)S(1)}, bf16[2,1,80,128]{3,2,1,0:T(8,128)(2,1)}, u32[]{:S(2)}) copy-start(bf16[2,1,80,128]{3,2,1,0:T(8,128)(2,1)} %param.4) | copy-start | bytes 122884
  11.9 29.4 %all-to-all-start = ((f32[2,1,80,480]{2,1,0,3:T(1,128)}), f32[2,1,80,480]{2,1,0,3:T(1,128)S(1)}, u32[]{:S(2)}, u32[]{:S(2)}) async-start(f32[2,1,80,480]{2,1,0,3:T(1,128)} %copy.38), calls=%async_computation | async-start | bytes 983040 | tf_op jit(solution)/shard_map/all_to_all | solution.py:114
  44.2 1.9 %copy-start = (f32[240,480]{1,0:T(8,128)S(1)}, f32[240,480]{1,0:T(8,128)}, u32[]{:S(2)}) copy-start(f32[240,480]{1,0:T(8,128)} %param.5) | copy-start | bytes 1382404
  58.9 10.4 %all-to-all-start.1 = ((f32[2,1,160,240]{3,1,0,2:T(1,128)}), f32[2,1,160,240]{3,1,0,2:T(1,128)S(1)}, u32[]{:S(2)}, u32[]{:S(2)}) async-start(f32[2,1,160,240]{3,1,0,2:T(1,128)} %copy.42), calls=%async_computation.1 | async-start | bytes 655360 | tf_op jit(solution)/shard_map/all_to_all | solution.py:116
